TPU v7x, 128 devices: a whole 4x4x4 slice. The times are simulated.
128 devices in a mesh: dp: 128 (over x, z, y, core).
Axes of the slice: x: 4, y: 4, z: 4, core: 2. Of those that a mesh axis runs over, the one named last changes fastest.
Arguments:
- token_ids: int32 [131072], P('dp'), may hold values from 0 to 31999, as said below
- tokens: bfloat16 [131072, 4096], P('dp'), may hold values from -64 to 64
- frozen_weight: bfloat16 [4096, 1024], replicated, may hold values from -0.09375 to 0.09375
- adapter_down: bfloat16 [4096, 128], replicated, may hold values from -0.09375 to 0.09375
- adapter_up: bfloat16 [128, 1024], replicated, may hold values from -1.5 to 1.5
- gate_weight: bfloat16 [4096, 8], replicated, may hold values from -1 to 1
- upstream: bfloat16 [131072, 1024], P('dp'), may hold values from -6 to 6
Outputs:
- projected: bfloat16 [131072, 1024], P('dp')
- input_grad: bfloat16 [131072, 4096], P('dp')
- clipped_down: float32 [4096, 128], replicated
- clipped_up: float32 [128, 1024], replicated
- clipped_gate: float32 [4096, 8], replicated
- load: float32 [8], replicated
- entropy: float32 [], replicated
Inputs may be any that keep to these rules, and one draw needn't show every extreme that they name: `token_ids`: within each device's block of 1024 tokens the live tokens (id not 0) come first, 256 or more of them, and padding (id 0) fills the rest; the last block is wholly live.
All inputs are finite; a program needn't handle non-finite values.
Results may differ from a plain program's by a relative error of at most 0.0095.
Values sent between devices are 32-bit elements; how exact they have to be, the bound alone decides.
A program may use at most 192 MiB of HBM per device.

v0:
```python
import math
import jax
import jax.numpy as jnp
from jax import lax
from jax.sharding import Mesh
from jax.sharding import PartitionSpec as P

DP = ("dp_0", "dp_1", "dp_2", "dp_3")


def over_axes(x, axes):
    for axis in axes:
        x = lax.psum(x, axis)
    return x


def left_dot(first, second):
    return lax.dot_general(
        first, second, (((0,), (0,)), ((), ())), preferred_element_type=jnp.float32
    )


def right_dot(first, second):
    return lax.dot_general(
        first, second, (((1,), (1,)), ((), ())), preferred_element_type=jnp.float32
    )


def exact_left(tokens, matrix):
    upper = matrix.astype(jnp.bfloat16)
    lower = (matrix - upper.astype(jnp.float32)).astype(jnp.bfloat16)
    return left_dot(tokens, upper) + left_dot(tokens, lower)


def share_stats(local):
    return (over_axes(local[0], DP), over_axes(local[1], DP), over_axes(local[2], DP))


def reduce_clip(terms, finish, limit):
    summed = lax.psum((terms[0], terms[1], terms[2]), DP)
    grads = finish(summed)
    total = (
        jnp.sum(grads[0] * grads[0]) + jnp.sum(grads[1] * grads[1]) + jnp.sum(grads[2] * grads[2])
    )
    factor = jnp.minimum(1.0, limit / jnp.sqrt(total))
    return (grads[0] * factor, grads[1] * factor, grads[2] * factor)


def on_device(token_ids, tokens, frozen_weight, adapter_down, adapter_up, gate_weight, upstream):
    width = tokens.shape[1]
    experts = gate_weight.shape[1]
    ranks = adapter_down.shape[1]
    rank = ranks // experts
    outputs = frozen_weight.shape[1]
    rows = tokens.shape[0]
    live = (token_ids != 0).astype(jnp.float32)
    base = jnp.dot(tokens, frozen_weight, preferred_element_type=jnp.float32)
    logits = jnp.dot(tokens, gate_weight, preferred_element_type=jnp.float32)
    prob = jax.nn.softmax(logits, axis=1)
    logp = jax.nn.log_softmax(logits, axis=1)
    low = jnp.dot(tokens, adapter_down, preferred_element_type=jnp.float32).astype(jnp.bfloat16)
    spread = jnp.repeat(prob, rank, axis=1)
    weighted = (low.astype(jnp.float32) * spread).astype(jnp.bfloat16)
    projected = (
        base + 2.0 * jnp.dot(weighted, adapter_up, preferred_element_type=jnp.float32)
    ).astype(jnp.bfloat16)
    masked = upstream * live.astype(jnp.bfloat16)[:, None]
    grad_up = 2.0 * left_dot(weighted, masked)
    back = right_dot(masked, adapter_up)
    gate_task = 2.0 * jnp.sum((low.astype(jnp.float32) * back).reshape(rows, experts, rank), axis=2)
    low_grad = (2.0 * spread * back).astype(jnp.bfloat16)
    grad_down = left_dot(tokens, low_grad)
    ent_tok = -jnp.sum(prob * logp, axis=1)
    local_stats = (jnp.sum(live[:, None] * prob, axis=0), jnp.sum(live * ent_tok), jnp.sum(live))

    def jac(vector):
        return prob * (vector - jnp.sum(prob * vector, axis=1, keepdims=True))

    plain_z = jac(gate_task) + 50.0 * live[:, None] * prob * (logp + ent_tok[:, None])
    frozen_back = right_dot(masked, frozen_weight) + right_dot(low_grad, adapter_down)
    count = width * ranks + ranks * outputs + width * experts
    limit = math.sqrt(count)
    load_all, ent_all, live_all = share_stats(local_stats)
    gate_z = plain_z + 2.0 * experts * 100.0 / live_all * live[:, None] * jac(load_all[None, :])
    terms = (grad_down, grad_up, exact_left(tokens, gate_z))

    def finish(summed):
        return summed

    clipped = reduce_clip(terms, finish, limit)
    input_grad = frozen_back + jnp.dot(
        gate_z, gate_weight.astype(jnp.float32).T, precision=lax.Precision.HIGHEST
    )
    return (
        projected,
        input_grad.astype(jnp.bfloat16),
        clipped[0],
        clipped[1],
        clipped[2],
        load_all / live_all,
        ent_all / live_all,
    )


def solution(mesh):
    torus = Mesh(mesh.devices.reshape(4, 4, 4, 2), ("dp_0", "dp_1", "dp_2", "dp_3"))
    return jax.shard_map(
        on_device,
        mesh=torus,
        in_specs=(P(DP), P(DP, None), P(), P(), P(), P(), P(DP, None)),
        out_specs=(P(DP, None), P(DP, None), P(), P(), P(), P(), P()),
        check_vma=False,
    )
```

profile of v0, /device:TPU:1, one launch (start us, length us, event | category | flops | bytes accessed | tf_op | source)
XLA Modules:
  0.0 243.0 jit_solution(7929073517609321213)
XLA Ops:
  7.2 0.0 copy-start
  7.2 0.0 all-reduce.7.cloned.1.call-start
  7.2 0.0 copy-start.1
  7.2 5.8 %fusion.21 = (f32[1024]{0:T(1024)S(1)}, f32[1024,8]{0,1:T(8,128)S(1)}) fusion(bf16[1024,4096]{1,0:T(8,128)(2,1)} %param.8, bf16[4096,8]{0,1:T(8,128)(2,1)} %param.12), kind=kOutput, calls=%fused_computation.48 | convolution fusion | flops 67116032 | bytes 8491008 | tf_op jit(solution)/shard_map/dot_general | solution.py:58
  13.1 0.0 copy-start.8
  13.1 0.0 copy-start.2
  13.1 0.0 copy-start.3
  13.2 0.0 copy-done
  13.2 0.1 copy-done.1
  13.3 2.9 %fusion.10 = f32[1024,128]{0,1:T(8,128)S(1)} fusion(bf16[1024,4096]{1,0:T(8,128)(2,1)S(1)} %copy-done.1, bf16[4096,128]{1,0:T(8,128)(2,1)S(1)} %copy-done), kind=kOutput, calls=%fused_computation.14 | convolution fusion | flops 1074003968 | bytes 9961472 | tf_op jit(solution)/shard_map/dot_general | solution.py:61
  16.2 0.0 copy-done.8
  16.2 0.0 copy-done.2
  16.3 0.0 copy-done.3
  16.3 1.5 fusion.16
  17.8 0.1 bitcast_reduce_fusion
  17.9 0.1 multiply_reduce_fusion.6
  18.0 0.6 select_reduce_fusion
  18.6 9.9 %all-reduce.3 = (f32[8]{0:T(128)S(1)}, f32[]{:T(128)}, f32[]{:T(128)}) all-reduce(f32[8]{0:T(128)S(1)} %get-tuple-element.16, f32[]{:T(128)} %get-tuple-element.18, f32[]{:T(128)} %get-tuple-element.17), channel_id=1, replica_groups=mesh['dp_0'=4,'dp_1'=4,'dp_2'=4,'dp_3'=2] {'dp_0'}, use_global_device_ids=true, to_apply=%region_11.12 | all-reduce | flops 10 | bytes 80 | tf_op jit(solution)/shard_map/psum | solution.py:13
  28.5 10.4 %all-reduce.2 = (f32[8]{0:T(128)S(1)}, f32[]{:T(128)}, f32[]{:T(128)}) all-reduce(f32[8]{0:T(128)S(1)} %get-tuple-element.28, f32[]{:T(128)} %get-tuple-element.29, f32[]{:T(128)} %get-tuple-element.30), channel_id=1, replica_groups=mesh['dp_0'=4,'dp_1'=4,'dp_2'=4,'dp_3'=2] {'dp_1'}, use_global_device_ids=true, to_apply=%region_12.13 | all-reduce | flops 10 | bytes 80 | tf_op jit(solution)/shard_map/psum | solution.py:13
  38.9 9.3 %all-reduce.1 = (f32[8]{0:T(128)S(1)}, f32[]{:T(128)}, f32[]{:T(128)}) all-reduce(f32[8]{0:T(128)S(1)} %get-tuple-element.25, f32[]{:T(128)} %get-tuple-element.26, f32[]{:T(128)} %get-tuple-element.27), channel_id=1, replica_groups=mesh['dp_0'=4,'dp_1'=4,'dp_2'=4,'dp_3'=2] {'dp_2'}, use_global_device_ids=true, to_apply=%region_13.14 | all-reduce | flops 10 | bytes 80 | tf_op jit(solution)/shard_map/psum | solution.py:13
  48.2 9.5 %all-reduce.4 = (f32[8]{0:T(128)S(1)}, f32[]{:T(128)}, f32[]{:T(128)}) all-reduce(f32[8]{0:T(128)S(1)} %get-tuple-element.22, f32[]{:T(128)} %get-tuple-element.23, f32[]{:T(128)} %get-tuple-element.24), channel_id=1, replica_groups=mesh['dp_0'=4,'dp_1'=4,'dp_2'=4,'dp_3'=2] {'dp_3'}, use_global_device_ids=true, to_apply=%region_14.15 | all-reduce | flops 10 | bytes 80 | tf_op jit(solution)/shard_map/psum | solution.py:13
  57.7 0.1 multiply_reduce_fusion.3
  58.4 0.0 copy-start.5
  58.5 6.0 %convolution_bitcast_fusion = f32[4096,128]{0,1:T(8,128)} fusion(bf16[1024,128]{0,1:T(8,128)(2,1)S(1)} %get-tuple-element.36, bf16[1024,4096]{1,0:T(8,128)(2,1)} %param.8), kind=kOutput, calls=%fused_computation.1 | convolution fusion | flops 1073741824 | bytes 10747904 | tf_op jit(solution)/shard_map/dot_general | solution.py:18
  64.5 0.0 copy-done.5
  64.5 0.0 slice-start
  64.5 1.3 fusion.7
  65.8 0.1 multiply_add_fusion
  65.9 0.0 slice-start.1
  65.9 4.7 %fusion.18 = f32[8,4096]{1,0:T(8,128)S(1)} fusion(bf16[1024,4096]{1,0:T(8,128)(2,1)} %param.8, f32[1024,8]{0,1:T(8,128)S(1)} %multiply_add_fusion), kind=kOutput, calls=%fused_computation.38 | convolution fusion | flops 67117056 | bytes 8552448 | tf_op jit(solution)/shard_map/dot_general | solution.py:18
  70.6 0.0 slice-done
  70.6 0.1 slice-done.1
  70.7 0.0 copy-start.7
  70.7 1.9 fusion
  72.6 0.0 all-reduce.7.cloned.1.call-update
  72.6 0.0 copy-done.7
  72.6 10.4 %fusion.23 = f32[1024,4096]{1,0:T(8,128)} fusion(f32[1024,8]{0,1:T(8,128)S(1)} %multiply_add_fusion, bf16[4096,8]{0,1:T(8,128)(2,1)S(1)} %copy-done.7), kind=kOutput, calls=%fused_computation.50 | convolution fusion | flops 402653184 | bytes 16875520 | tf_op jit(solution)/shard_map/dot_general | solution.py:91
  83.0 12.7 %fusion.22 = f32[1024,1024]{1,0:T(8,128)S(1)} fusion(bf16[1024,4096]{1,0:T(8,128)(2,1)} %param.8, bf16[4096,1024]{1,0:T(8,128)(2,1)} %param.9), kind=kOutput, calls=%fused_computation.49 | convolution fusion | flops 8589934592 | bytes 20971520 | tf_op jit(solution)/shard_map/dot_general | solution.py:57
  95.7 0.0 copy-start.4
  95.7 0.0 copy-start.6
  95.8 14.6 %fusion.5 = f32[1024,4096]{1,0:T(8,128)} fusion(bf16[4096,1024]{1,0:T(8,128)(2,1)} %param.9, bf16[1024,1024]{1,0:T(8,128)(2,1)S(1)} %copy-done.2, bf16[1024]{0:T(1024)(128)(2,1)S(1)} %get-tuple-element.41), kind=kOutput, calls=%fused_computation.10 | convolution fusion | flops 8590983168 | bytes 27265024 | tf_op jit(solution)/shard_map/dot_general | solution.py:24
  110.3 1.2 broadcast_divide_fusion
  111.5 0.0 copy-done.4
  111.5 0.0 copy-done.6
  111.5 2.1 add_convert_fusion.1
  114.9 15.4 %add_convert_fusion = bf16[1024,4096]{1,0:T(8,128)(2,1)} fusion(f32[1024,4096]{1,0:T(8,128)} %fusion.23, f32[1024,4096]{1,0:T(8,128)} %fusion.5, bf16[1024,128]{0,1:T(8,128)(2,1)S(1)} %get-tuple-element.36, bf16[4096,128]{1,0:T(8,128)(2,1)S(1)} %copy-done), kind=kOutput, calls=%fused_computation | convolution fusion | flops 1086324736 | bytes 43253760 | tf_op jit(solution)/shard_map/dot_general | solution.py:24
  130.3 89.6 %all-reduce.7.cloned.1.call-done = (f32[4096,128]{0,1:T(8,128)}, f32[128,1024]{1,0:T(8,128)}, f32[4096,8]{0,1:T(8,128)}) async-done(((f32[4096,128]{0,1:T(8,128)}, f32[128,1024]{1,0:T(8,128)}, f32[4096,8]{0,1:T(8,128)}), (f32[4096,128]{0,1:T(8,128)}, f32[128,1024]{1,0:T(8,128)}, f32[4096,8]{0,1:T(8,128)})) %all-reduce.7.cloned.1.call-update) | async-done | bytes 2752528 | tf_op jit(solution)/shard_map/psum | solution.py:40
  219.9 2.7 %multiply_reduce_fusion = f32[]{:T(128)} fusion(f32[4096,128]{0,1:T(8,128)} %get-tuple-element.19), kind=kLoop, calls=%fused_computation.5 | loop fusion | flops 1048575 | bytes 2097156 | tf_op jit(solution)/shard_map/reduce_sum | solution.py:43
  222.6 1.8 multiply_reduce_fusion.1
  224.4 1.5 multiply_reduce_fusion.2
  227.9 1.8 broadcast_multiply_fusion
  229.7 1.9 broadcast_multiply_fusion.1
  231.6 1.6 broadcast_multiply_fusion.2
  233.2 1.8 copy.14
  (7 shorter events, 0.1 us)
Async XLA Ops:
  7.2 6.0 %copy-start = (bf16[4096,128]{1,0:T(8,128)(2,1)S(1)}, bf16[4096,128]{1,0:T(8,128)(2,1)}, u32[]{:S(2)}) copy-start(bf16[4096,128]{1,0:T(8,128)(2,1)} %param.10) | copy-start | bytes 3145732
  7.2 212.7 %all-reduce.7.cloned.1.call-start = ((), (), s32[]{:S(2)}) async-start(), calls=%async_computation | async-start | bytes 5505024 | tf_op jit(solution)/shard_map/psum | solution.py:40
  7.2 6.1 %copy-start.1 = (bf16[1024,4096]{1,0:T(8,128)(2,1)S(1)}, bf16[1024,4096]{1,0:T(8,128)(2,1)}, u32[]{:S(2)}) copy-start(bf16[1024,4096]{1,0:T(8,128)(2,1)} %param.8) | copy-start | bytes 25165828
  13.1 3.2 %copy-start.8 = (s32[1024]{0:T(1024)S(1)}, s32[1024]{0:T(1024)}, u32[]{:S(2)}) copy-start(s32[1024]{0:T(1024)} %param.7) | copy-start | bytes 12292
  13.1 3.2 %copy-start.2 = (bf16[1024,1024]{1,0:T(8,128)(2,1)S(1)}, bf16[1024,1024]{1,0:T(8,128)(2,1)}, u32[]{:S(2)}) copy-start(bf16[1024,1024]{1,0:T(8,128)(2,1)} %param.13) | copy-start | bytes 6291460
  13.1 3.2 %copy-start.3 = (bf16[128,1024]{1,0:T(8,128)(2,1)S(1)}, bf16[128,1024]{1,0:T(8,128)(2,1)}, u32[]{:S(2)}) copy-start(bf16[128,1024]{1,0:T(8,128)(2,1)} %param.11) | copy-start | bytes 786436
  58.4 6.0 %copy-start.5 = (bf16[1024,128]{0,1:T(8,128)(2,1)S(1)}, bf16[1024,128]{0,1:T(8,128)(2,1)}, u32[]{:S(2)}) copy-start(bf16[1024,128]{0,1:T(8,128)(2,1)} %get-tuple-element.38) | copy-start | bytes 786436
  64.5 6.1 %slice-start = ((s8[8388608]{0:T(1024)(128)(4,1)}), s8[4194304]{0:T(1024)(128)(4,1)S(1)}, s32[]{:S(2)}) async-start(s8[8388608]{0:T(1024)(128)(4,1)} %bitcast.34), calls=%async_computation.1 | async-start | bytes 8388608
  65.9 4.9 %slice-start.1 = ((s8[8388608]{0:T(1024)(128)(4,1)}), s8[4194304]{0:T(1024)(128)(4,1)S(1)}, s32[]{:S(2)}) async-start(s8[8388608]{0:T(1024)(128)(4,1)} %bitcast.34), calls=%async_computation.2 | async-start | bytes 8388608
  70.7 1.9 copy-start.7
  95.7 15.8 %copy-start.4 = (bf16[128,1024]{1,0:T(8,128)(2,1)S(1)}, bf16[128,1024]{1,0:T(8,128)(2,1)}, u32[]{:S(2)}) copy-start(bf16[128,1024]{1,0:T(8,128)(2,1)} %param.11) | copy-start | bytes 786436
  95.7 15.7 %copy-start.6 = (bf16[1024,128]{0,1:T(8,128)(2,1)S(1)}, bf16[1024,128]{0,1:T(8,128)(2,1)}, u32[]{:S(2)}) copy-start(bf16[1024,128]{0,1:T(8,128)(2,1)} %get-tuple-element.38) | copy-start | bytes 786436
Sparse Core Ops, SparseCore 0:
  72.7 147.1 all-reduce.6
where the time goes:
time: 243 us
  waiting for transfers between devices  89.6 us (37%)
  matrix products  79.3 us (33%)
  blocking collectives  39.1 us (16%)
  between operations  19.4 us (8%)
  other arithmetic  13.5 us (6%)
    psum x1, waiting for transfers between devices, reduce_clip(): summed = lax.psum((terms[0], terms[1], terms[2]), DP)  89.6 us
    psum x4, blocking collectives, over_axes(): x = lax.psum(x, axis)  39.1 us
    dot_general x3, matrix products, right_dot(): lax.dot_general(first, second, (((1,), (1,)), ((), ())), preferred_elemen...  31.5 us
    dot_general x4, matrix products, left_dot(): lax.dot_general(first, second, (((0,), (0,)), ((), ())), preferred_elemen...  13.9 us
    dot_general x1, matrix products, on_device(): base = jnp.dot(tokens, frozen_weight, preferred_element_type=jnp.float32)  12.7 us
    dot_general x1, matrix products, on_device(): jnp.dot(gate_z, gate_weight.astype(jnp.float32).T, precision=lax.Precisio...  10.4 us
    dot_general x1, matrix products, on_device(): logits = jnp.dot(tokens, gate_weight, preferred_element_type=jnp.float32)  5.81 us
    mul x3, other arithmetic, reduce_clip(): return (grads[0] * factor, grads[1] * factor, grads[2] * factor)  5.23 us
  transfers between devices with their start and end apart: 1, of which 1 were waited for; matrix products, arithmetic and copies ran while one was open for 23% of the time, Pallas kernels for 0%

commit v1 on v0

--- a/solution.py
+++ b/solution.py
@@ -10,7 +10,7 @@
 
 def over_axes(x, axes):
     for axis in axes:
-        x = lax.psum(x, axis)
+        x = lax.all_gather(x, axis_name=axis).sum(axis=0)
     return x
 
 

time: 243 us -> 263 us (1.082)
  local copies, waits for them, and re-layouts: 2.14 us -> 17.5 us
  other arithmetic: 13.5 us -> 18.4 us
    psum x4 -> x0, blocking collectives: 39.1 us -> none  [over_axes(): x = lax.psum(x, axis)]
    unnamed x0 -> x4, blocking collectives: none -> 36.5 us
    unnamed x23 -> x57, local copies, waits for them, and re-layouts: 2.14 us -> 17.2 us
    reduce_sum x0 -> x12, other arithmetic: none -> 4.88 us  [over_axes(): x = lax.all_gather(x, axis_name=axis).sum(axis=0)]
  transfers between devices with their start and end apart: 1 -> 1, of which waited for: 1 -> 1; matrix products, arithmetic and copies ran while one was open for 23% -> 22% of each run, Pallas kernels for 0% -> 0%
where the time goes in v1:
time: 263 us
  waiting for transfers between devices  89 us (34%)
  matrix products  79.3 us (30%)
  blocking collectives  36.5 us (14%)
  between operations  22 us (8%)
  other arithmetic  18.4 us (7%)
  local copies, waits for them, and re-layouts  17.5 us (7%)
    psum x1, waiting for transfers between devices, reduce_clip(): summed = lax.psum((terms[0], terms[1], terms[2]), DP)  89 us
    unnamed x4, blocking collectives  36.5 us
    dot_general x3, matrix products, right_dot(): lax.dot_general(first, second, (((1,), (1,)), ((), ())), preferred_elemen...  31.5 us
    unnamed x57, local copies, waits for them, and re-layouts  17.2 us
    dot_general x4, matrix products, left_dot(): lax.dot_general(first, second, (((0,), (0,)), ((), ())), preferred_elemen...  13.9 us
    dot_general x1, matrix products, on_device(): base = jnp.dot(tokens, frozen_weight, preferred_element_type=jnp.float32)  12.7 us
    dot_general x1, matrix products, on_device(): jnp.dot(gate_z, gate_weight.astype(jnp.float32).T, precision=lax.Precisio...  10.4 us
    dot_general x1, matrix products, on_device(): logits = jnp.dot(tokens, gate_weight, preferred_element_type=jnp.float32)  5.81 us
  transfers between devices with their start and end apart: 1, of which 1 were waited for; matrix products, arithmetic and copies ran while one was open for 22% of the time, Pallas kernels for 0%

profile of v1, /device:TPU:1, one launch (start us, length us, event | category | flops | bytes accessed | tf_op | source)
XLA Modules:
  0.0 262.7 jit_solution(10274909654023047768)
XLA Ops:
  7.2 0.0 copy-start
  7.2 0.0 all-reduce.19.cloned.1.call-start
  7.2 0.0 copy-start.1
  7.2 5.8 %fusion.21 = (f32[1024]{0:T(1024)S(1)}, f32[1024,8]{0,1:T(8,128)S(1)}) fusion(bf16[1024,4096]{1,0:T(8,128)(2,1)} %param.8, bf16[4096,8]{0,1:T(8,128)(2,1)} %param.12), kind=kOutput, calls=%fused_computation.48 | convolution fusion | flops 67116032 | bytes 8491008 | tf_op jit(solution)/shard_map/dot_general | solution.py:58
  13.2 0.1 copy-done.1
  13.3 2.9 %fusion.10 = f32[1024,128]{0,1:T(8,128)S(1)} fusion(bf16[1024,4096]{1,0:T(8,128)(2,1)S(1)} %copy-done.1, bf16[4096,128]{1,0:T(8,128)(2,1)S(1)} %copy-done), kind=kOutput, calls=%fused_computation.14 | convolution fusion | flops 1074003968 | bytes 9961472 | tf_op jit(solution)/shard_map/dot_general | solution.py:61
  16.3 1.5 fusion.16
  17.8 0.1 bitcast_reduce_fusion
  17.9 0.1 multiply_reduce_fusion.6
  18.0 0.6 select_reduce_fusion
  18.6 1.2 dynamic-slice
  20.5 1.4 dynamic-update-slice
  21.9 1.4 dynamic-update-slice.8
  23.3 0.2 dynamic-update-slice.4
  23.5 9.3 %all-reduce.15 = (f32[32]{0:T(128)S(1)}, f32[4]{0:T(128)S(1)}, f32[4]{0:T(128)S(1)}) all-reduce(f32[32]{0:T(128)S(1)} %dynamic-update-slice.4, f32[4]{0:T(128)S(1)} %dynamic-update-slice, f32[4]{0:T(128)S(1)} %dynamic-update-slice.8), channel_id=2, replica_groups=mesh['dp_0'=4,'dp_1'=4,'dp_2'=4,'dp_3'=2] {'dp_0'}, use_global_device_ids=true, to_apply=%add.4 | all-reduce | flops 40 | bytes 320
  32.8 0.1 reshape.40
  32.9 0.6 dynamic-slice.1
  34.1 0.6 reduce_sum.217
  34.7 0.6 reduce_sum.231
  35.3 1.4 dynamic-update-slice.1
  36.7 1.4 dynamic-update-slice.9
  38.1 0.2 dynamic-update-slice.5
  38.3 9.7 %all-reduce.14 = (f32[32]{0:T(128)S(1)}, f32[4]{0:T(128)S(1)}, f32[4]{0:T(128)S(1)}) all-reduce(f32[32]{0:T(128)S(1)} %dynamic-update-slice.5, f32[4]{0:T(128)S(1)} %dynamic-update-slice.1, f32[4]{0:T(128)S(1)} %dynamic-update-slice.9), channel_id=3, replica_groups=mesh['dp_0'=4,'dp_1'=4,'dp_2'=4,'dp_3'=2] {'dp_1'}, use_global_device_ids=true, to_apply=%add.5 | all-reduce | flops 40 | bytes 320
  48.1 0.1 reshape.41
  48.1 0.6 dynamic-slice.2
  49.4 0.6 reduce_sum.218
  50.0 0.6 reduce_sum.232
  50.6 1.4 dynamic-update-slice.2
  52.0 1.4 dynamic-update-slice.10
  53.4 0.2 dynamic-update-slice.6
  53.6 8.7 %all-reduce.13 = (f32[32]{0:T(128)S(1)}, f32[4]{0:T(128)S(1)}, f32[4]{0:T(128)S(1)}) all-reduce(f32[32]{0:T(128)S(1)} %dynamic-update-slice.6, f32[4]{0:T(128)S(1)} %dynamic-update-slice.2, f32[4]{0:T(128)S(1)} %dynamic-update-slice.10), channel_id=4, replica_groups=mesh['dp_0'=4,'dp_1'=4,'dp_2'=4,'dp_3'=2] {'dp_2'}, use_global_device_ids=true, to_apply=%add.6 | all-reduce | flops 40 | bytes 320
  62.3 0.1 reshape.42
  62.4 0.6 dynamic-slice.3
  63.7 0.6 reduce_sum.219
  64.3 0.6 reduce_sum.233
  64.9 1.4 dynamic-update-slice.3
  66.3 1.4 dynamic-update-slice.11
  67.7 0.2 dynamic-update-slice.7
  67.9 8.8 %all-reduce.16 = (f32[16]{0:T(128)S(1)}, f32[2]{0:T(128)S(1)}, f32[2]{0:T(128)S(1)}) all-reduce(f32[16]{0:T(128)S(1)} %dynamic-update-slice.7, f32[2]{0:T(128)S(1)} %dynamic-update-slice.3, f32[2]{0:T(128)S(1)} %dynamic-update-slice.11), channel_id=5, replica_groups=mesh['dp_0'=4,'dp_1'=4,'dp_2'=4,'dp_3'=2] {'dp_3'}, use_global_device_ids=true, to_apply=%add.7 | all-reduce | flops 20 | bytes 160
  76.7 0.1 reshape.43
  76.8 0.1 multiply_reduce_fusion.3
  76.9 0.6 reduce_sum.220
  78.2 6.0 %convolution_bitcast_fusion = f32[4096,128]{0,1:T(8,128)} fusion(bf16[1024,128]{0,1:T(8,128)(2,1)S(1)} %get-tuple-element.36, bf16[1024,4096]{1,0:T(8,128)(2,1)} %param.8), kind=kOutput, calls=%fused_computation.1 | convolution fusion | flops 1073741824 | bytes 10747904 | tf_op jit(solution)/shard_map/dot_general | solution.py:18
  84.2 1.3 fusion.7
  85.5 0.1 multiply_add_fusion
  85.6 4.7 %fusion.18 = f32[8,4096]{1,0:T(8,128)S(1)} fusion(bf16[1024,4096]{1,0:T(8,128)(2,1)} %param.8, f32[1024,8]{0,1:T(8,128)S(1)} %multiply_add_fusion), kind=kOutput, calls=%fused_computation.38 | convolution fusion | flops 67117056 | bytes 8552448 | tf_op jit(solution)/shard_map/dot_general | solution.py:18
  90.3 0.1 slice-done.1
  90.5 1.9 fusion
  92.3 0.0 all-reduce.19.cloned.1.call-update
  92.4 10.4 %fusion.23 = f32[1024,4096]{1,0:T(8,128)} fusion(f32[1024,8]{0,1:T(8,128)S(1)} %multiply_add_fusion, bf16[4096,8]{0,1:T(8,128)(2,1)S(1)} %copy-done.7), kind=kOutput, calls=%fused_computation.50 | convolution fusion | flops 402653184 | bytes 16875520 | tf_op jit(solution)/shard_map/dot_general | solution.py:91
  102.7 12.7 %fusion.22 = f32[1024,1024]{1,0:T(8,128)S(1)} fusion(bf16[1024,4096]{1,0:T(8,128)(2,1)} %param.8, bf16[4096,1024]{1,0:T(8,128)(2,1)} %param.9), kind=kOutput, calls=%fused_computation.49 | convolution fusion | flops 8589934592 | bytes 20971520 | tf_op jit(solution)/shard_map/dot_general | solution.py:57
  115.5 14.6 %fusion.5 = f32[1024,4096]{1,0:T(8,128)} fusion(bf16[4096,1024]{1,0:T(8,128)(2,1)} %param.9, bf16[1024,1024]{1,0:T(8,128)(2,1)S(1)} %copy-done.2, bf16[1024]{0:T(1024)(128)(2,1)S(1)} %get-tuple-element.41), kind=kOutput, calls=%fused_computation.10 | convolution fusion | flops 8590983168 | bytes 27265024 | tf_op jit(solution)/shard_map/dot_general | solution.py:24
  130.1 1.2 broadcast_divide_fusion
  131.2 2.1 add_convert_fusion.1
  133.3 0.6 reduce_sum.234
  135.2 15.4 %add_convert_fusion = bf16[1024,4096]{1,0:T(8,128)(2,1)} fusion(f32[1024,4096]{1,0:T(8,128)} %fusion.23, f32[1024,4096]{1,0:T(8,128)} %fusion.5, bf16[1024,128]{0,1:T(8,128)(2,1)S(1)} %get-tuple-element.36, bf16[4096,128]{1,0:T(8,128)(2,1)S(1)} %copy-done), kind=kOutput, calls=%fused_computation | convolution fusion | flops 1086324736 | bytes 43253760 | tf_op jit(solution)/shard_map/dot_general | solution.py:24
  150.7 89.0 %all-reduce.19.cloned.1.call-done = (f32[4096,128]{0,1:T(8,128)}, f32[128,1024]{1,0:T(8,128)}, f32[4096,8]{0,1:T(8,128)}) async-done(((f32[4096,128]{0,1:T(8,128)}, f32[128,1024]{1,0:T(8,128)}, f32[4096,8]{0,1:T(8,128)}), (f32[4096,128]{0,1:T(8,128)}, f32[128,1024]{1,0:T(8,128)}, f32[4096,8]{0,1:T(8,128)})) %all-reduce.19.cloned.1.call-update) | async-done | bytes 2752528 | tf_op jit(solution)/shard_map/psum | solution.py:40
  239.6 2.7 %multiply_reduce_fusion = f32[]{:T(128)} fusion(f32[4096,128]{0,1:T(8,128)} %get-tuple-element.19), kind=kLoop, calls=%fused_computation.5 | loop fusion | flops 1048575 | bytes 2097156 | tf_op jit(solution)/shard_map/reduce_sum | solution.py:43
  242.4 1.8 multiply_reduce_fusion.1
  244.2 1.5 multiply_reduce_fusion.2
  247.7 1.8 broadcast_multiply_fusion
  249.5 1.9 broadcast_multiply_fusion.1
  251.4 1.6 broadcast_multiply_fusion.2
  252.9 1.8 copy.14
  (47 shorter events, 0.2 us)
Async XLA Ops:
  7.2 6.0 %copy-start = (bf16[4096,128]{1,0:T(8,128)(2,1)S(1)}, bf16[4096,128]{1,0:T(8,128)(2,1)}, u32[]{:S(2)}) copy-start(bf16[4096,128]{1,0:T(8,128)(2,1)} %param.10) | copy-start | bytes 3145732
  7.2 232.5 %all-reduce.19.cloned.1.call-start = ((), (), s32[]{:S(2)}) async-start(), calls=%async_computation | async-start | bytes 5505024 | tf_op jit(solution)/shard_map/psum | solution.py:40
  7.2 6.1 %copy-start.1 = (bf16[1024,4096]{1,0:T(8,128)(2,1)S(1)}, bf16[1024,4096]{1,0:T(8,128)(2,1)}, u32[]{:S(2)}) copy-start(bf16[1024,4096]{1,0:T(8,128)(2,1)} %param.8) | copy-start | bytes 25165828
  13.1 3.2 %copy-start.8 = (s32[1024]{0:T(1024)S(1)}, s32[1024]{0:T(1024)}, u32[]{:S(2)}) copy-start(s32[1024]{0:T(1024)} %param.7) | copy-start | bytes 12292
  13.1 3.2 %copy-start.2 = (bf16[1024,1024]{1,0:T(8,128)(2,1)S(1)}, bf16[1024,1024]{1,0:T(8,128)(2,1)}, u32[]{:S(2)}) copy-start(bf16[1024,1024]{1,0:T(8,128)(2,1)} %param.13) | copy-start | bytes 6291460
  13.1 3.2 %copy-start.3 = (bf16[128,1024]{1,0:T(8,128)(2,1)S(1)}, bf16[128,1024]{1,0:T(8,128)(2,1)}, u32[]{:S(2)}) copy-start(bf16[128,1024]{1,0:T(8,128)(2,1)} %param.11) | copy-start | bytes 786436
  13.3 19.6 %copy-start.11 = (u32[128]{0:T(128)S(1)}, u32[128]{0:T(128)}, u32[]{:S(2)}) copy-start(u32[128]{0:T(128)} %constant.36) | copy-start | bytes 1540
  13.3 34.8 %copy-start.10 = (u32[128]{0:T(128)S(1)}, u32[128]{0:T(128)}, u32[]{:S(2)}) copy-start(u32[128]{0:T(128)} %constant.41) | copy-start | bytes 1540
  13.3 49.1 %copy-start.9 = (u32[128]{0:T(128)S(1)}, u32[128]{0:T(128)}, u32[]{:S(2)}) copy-start(u32[128]{0:T(128)} %constant.46) | copy-start | bytes 1540
  78.2 6.0 %copy-start.5 = (bf16[1024,128]{0,1:T(8,128)(2,1)S(1)}, bf16[1024,128]{0,1:T(8,128)(2,1)}, u32[]{:S(2)}) copy-start(bf16[1024,128]{0,1:T(8,128)(2,1)} %get-tuple-element.38) | copy-start | bytes 786436
  84.2 6.1 %slice-start = ((s8[8388608]{0:T(1024)(128)(4,1)}), s8[4194304]{0:T(1024)(128)(4,1)S(1)}, s32[]{:S(2)}) async-start(s8[8388608]{0:T(1024)(128)(4,1)} %bitcast.50), calls=%async_computation.1 | async-start | bytes 8388608
  85.6 4.9 %slice-start.1 = ((s8[8388608]{0:T(1024)(128)(4,1)}), s8[4194304]{0:T(1024)(128)(4,1)S(1)}, s32[]{:S(2)}) async-start(s8[8388608]{0:T(1024)(128)(4,1)} %bitcast.50), calls=%async_computation.2 | async-start | bytes 8388608
  90.5 1.9 copy-start.7
  115.5 15.8 %copy-start.4 = (bf16[128,1024]{1,0:T(8,128)(2,1)S(1)}, bf16[128,1024]{1,0:T(8,128)(2,1)}, u32[]{:S(2)}) copy-start(bf16[128,1024]{1,0:T(8,128)(2,1)} %param.11) | copy-start | bytes 786436
  115.5 15.7 %copy-start.6 = (bf16[1024,128]{0,1:T(8,128)(2,1)S(1)}, bf16[1024,128]{0,1:T(8,128)(2,1)}, u32[]{:S(2)}) copy-start(bf16[1024,128]{0,1:T(8,128)(2,1)} %get-tuple-element.38) | copy-start | bytes 786436
Sparse Core Ops, SparseCore 0:
  92.5 147.1 all-reduce.18
